TPU v7x, 8 devices: a whole 2x2x1 slice. The times are simulated.
8 devices in a mesh: dp: 2 (over z, y), ep: 4 (over x, core).
Axes of the slice: x: 2, y: 2, z: 1, core: 2. Of those that a mesh axis runs over, the one named last changes fastest.
Arguments:
- tokens: bfloat16 [8192, 768], P(('dp', 'ep')), parts along dimension 0
- choice_idx: int32 [64, 128], P(('dp', 'ep')), parts along dimension 0
- gate_weight: float32 [64, 128], P(('dp', 'ep')), parts along dimension 0
- w_in: bfloat16 [32, 768, 3072], P('ep')
- w_out: bfloat16 [32, 3072, 768], P('ep')
Outputs:
- output: bfloat16 [8192, 768], P(('dp', 'ep')), parts along dimension 0
There are 2 independent parts. A program takes and returns all parts, laid end to end along the dimension named above; an argument that names none is the same for every part.
All inputs are finite; a program needn't handle non-finite values.
Results may differ from a plain program's by a relative error of at most 0.001.
Values are sent between devices in bfloat16 or wider.
A program may use at most 1 GiB of HBM per device.

v0:
```python
import jax
import jax.numpy as jnp
from jax import lax
from jax.sharding import PartitionSpec as P


def solution(mesh):
    group_n = mesh.shape["ep"]
    row_spec = P(("dp", "ep"), None)
    expert_spec = P("ep", None, None)

    def local_layer(tok_loc, sel_loc, gate_loc, win_loc, wout_loc):
        tok_count, model_dim = tok_loc.shape
        exp_count, cap_slots = sel_loc.shape
        slot_total = exp_count * cap_slots
        pair_cap = 2 * slot_total // group_n
        flat_sel = sel_loc.reshape(slot_total)
        src_dev = flat_sel // tok_count
        src_row = flat_sel % tok_count
        slot_order = jnp.argsort(src_dev, stable=True)
        counts = jax.ops.segment_sum(jnp.ones_like(src_dev), src_dev, num_segments=group_n)
        starts = jnp.cumsum(counts) - counts
        lane_idx = jnp.arange(pair_cap, dtype=jnp.int32)
        is_valid = lane_idx[None, :] < counts[:, None]
        slot_of = slot_order[jnp.minimum(starts[:, None] + lane_idx[None, :], slot_total - 1)]
        request = jnp.where(is_valid, src_row[slot_of], 0)
        sorted_rank = jnp.zeros(slot_total, jnp.int32).at[slot_order].set(jnp.arange(slot_total, dtype=jnp.int32))
        recv_place = src_dev * pair_cap + sorted_rank - starts[src_dev]
        asked_rows = lax.all_to_all(request, "ep", 0, 0, tiled=True)
        send_rows = tok_loc[asked_rows]
        got_rows = lax.all_to_all(send_rows, "ep", 0, 0, tiled=True)
        expert_in = got_rows.reshape(group_n * pair_cap, model_dim)[recv_place].reshape(exp_count, cap_slots, model_dim)
        pre_act = jnp.einsum("ecd,edf->ecf", expert_in, win_loc, preferred_element_type=jnp.float32)
        hidden = jax.nn.gelu(pre_act, approximate=True).astype(jnp.bfloat16)
        expert_out = jnp.einsum("ecf,efd->ecd", hidden, wout_loc, preferred_element_type=jnp.float32)
        weighted = (gate_loc[:, :, None] * expert_out).astype(jnp.bfloat16).reshape(slot_total, model_dim)
        back_rows = jnp.where(is_valid[:, :, None], weighted[slot_of], jnp.zeros((), jnp.bfloat16))
        returned = lax.all_to_all(back_rows, "ep", 0, 0, tiled=True)
        added = jax.ops.segment_sum(returned.reshape(group_n * pair_cap, model_dim).astype(jnp.float32), asked_rows.reshape(group_n * pair_cap), num_segments=tok_count)
        return (tok_loc.astype(jnp.float32) + added).astype(jnp.bfloat16)

    return jax.shard_map(local_layer, mesh=mesh, in_specs=(row_spec, row_spec, row_spec, expert_spec, expert_spec), out_specs=row_spec, check_vma=False)
```

profile of v0, /device:TPU:0, one launch (start us, length us, event | category | flops | bytes accessed | tf_op | source)
XLA Modules:
  0.0 205.4 jit_solution(17136537622412069119)
XLA Ops:
  0.0 0.7 add_select_fusion
  0.7 0.7 and_select_fusion
  1.4 7.6 %scatter_custom_fusion = s32[4]{0:T(128)S(1)} fusion(s32[1024]{0:T(1024)S(1)} %bitcast.71, s32[1024]{0:T(1024)S(1)} %broadcast.241, s32[]{:T(128)} %constant.18.clone.1), kind=kCustom, calls=%fused_computation.58 | custom fusion | flops 1024 | bytes 20 | tf_op jit(solution)/shard_map/scatter-add | solution.py:21
  9.0 0.2 reduce-window.9
  9.2 0.7 fusion.30
  9.9 0.1 compare_select_fusion.2
  10.0 4.4 %sort.17 = (s32[1024]{0:T(1024)}, s32[1024]{0:T(1024)S(1)}) sort(s32[1024]{0:T(1024)S(1)} %add_select_fusion, s32[1024]{0:T(1024)S(1)} %iota.20), dimensions={0}, to_apply=%region_1.2 | sort | flops 10240 | bytes 16384 | tf_op jit(solution)/shard_map/jit(argsort)/sort | solution.py:20
  14.4 0.0 copy-start.4
  14.4 8.6 %gather_fusion = s32[2048]{0:T(1024)S(1)} fusion(s32[1024]{0:T(1024)S(1)} %get-tuple-element.6, s32[2048]{0:T(1024)S(1)} %broadcast_clamp_fusion.1), kind=kCustom, calls=%fused_computation | custom fusion | bytes 24576 | tf_op jit(solution)/shard_map/gather | solution.py:25
  23.0 0.0 copy-start.2
  23.0 4.3 %scatter_custom_fusion.1 = s32[1024]{0:T(1024)S(1)} fusion(s32[1024]{0:T(1024)S(1)} %compare_select_fusion.9, s32[1024]{0:T(1024)S(1)} %iota.21, s32[]{:T(128)} %constant.18.clone.1), kind=kCustom, calls=%fused_computation.55 | custom fusion | bytes 4100 | tf_op jit(solution)/shard_map/scatter | solution.py:27
  27.3 0.0 copy-done.4
  27.3 2.5 %compare_select_fusion.5 = s32[1024,1]{0,1:T(1,128)S(1)} fusion(s32[]{:T(128)} %bitcast.14, s32[]{:T(128)} %bitcast.15, s32[]{:T(128)} %bitcast.17, s32[]{:T(128)} %bitcast.16, s32[1024,1]{0,1:T(1,128)S(1)} %bitcast.63), kind=kLoop, calls=%fused_computation.31 | loop fusion | flops 24576 | bytes 8208 | tf_op jit(solution)/shard_map/gather | solution.py:28
  29.9 0.0 copy-start
  29.9 8.6 %gather_fusion.1 = s32[2048]{0:T(1024)S(1)} fusion(s32[1024]{0:T(1024)S(1)} %get-tuple-element.8, s32[2048]{0:T(1024)S(1)} %broadcast_clamp_fusion.2), kind=kCustom, calls=%fused_computation.1 | custom fusion | bytes 24576 | tf_op jit(solution)/shard_map/gather | solution.py:26
  38.5 0.0 copy-done.2
  38.5 0.1 compare_select_fusion.3
  38.6 8.2 %all_to_all.19 = s32[4,1,512]{2,1,0:T(1,128)S(1)} all-to-all(s32[4,1,512]{2,1,0:T(1,128)S(1)} %compare_select_fusion.3), channel_id=1, replica_groups=mesh['dp'=2,'ep'=4] {'ep'}, dimensions={0} | all-to-all | bytes 16384 | tf_op jit(solution)/shard_map/all_to_all | solution.py:29
  46.8 0.0 copy-start.5
  46.8 0.6 copy-done.5
  47.4 0.0 copy-done
  47.5 9.4 %gather_fusion.2 = bf16[2048,768]{1,0:T(8,128)(2,1)} fusion(bf16[1024,768]{1,0:T(8,128)(2,1)S(1)} %copy-done, s32[2048]{0:T(1024)S(1)} %broadcast_clamp_fusion), kind=kCustom, calls=%fused_computation.2 | custom fusion | bytes 6299648 | tf_op jit(solution)/shard_map/gather | solution.py:30
  56.8 3.7 %all-to-all-start.1 = ((bf16[4,512,768]{2,1,0:T(8,128)(2,1)}), bf16[4,512,768]{2,1,0:T(8,128)(2,1)S(1)}, u32[]{:S(2)}, u32[]{:S(2)}) async-start(bf16[4,512,768]{2,1,0:T(8,128)(2,1)} %bitcast.59), calls=%async_computation.1 | async-start | bytes 6291456 | tf_op jit(solution)/shard_map/all_to_all | solution.py:31
  60.5 0.6 iota_compare_fusion
  61.2 36.0 %all-to-all-done.1 = bf16[4,512,768]{2,1,0:T(8,128)(2,1)S(1)} async-done(((bf16[4,512,768]{2,1,0:T(8,128)(2,1)}), bf16[4,512,768]{2,1,0:T(8,128)(2,1)S(1)}, u32[]{:S(2)}, u32[]{:S(2)}) %all-to-all-start.1) | async-done | bytes 3145760 | tf_op jit(solution)/shard_map/all_to_all | solution.py:31
  97.2 0.0 copy-start.7
  97.2 5.2 %gather_fusion.3 = bf16[1024,768]{1,0:T(8,128)(2,1)} fusion(bf16[2048,768]{1,0:T(8,128)(2,1)S(1)} %bitcast.58, s32[1024]{0:T(1024)S(1)} %get-tuple-element.7), kind=kCustom, calls=%fused_computation.3 | custom fusion | bytes 3149824 | tf_op jit(solution)/shard_map/gather | solution.py:32
  102.4 0.0 copy-done.7
  102.4 0.0 copy-start.3
  102.4 27.0 %multiply_convert_fusion = bf16[8,128,768]{2,1,0:T(8,128)(2,1)S(1)} fusion(bf16[8,3072,768]{2,1,0:T(8,128)(2,1)} %param.9, f32[8,128]{1,0:T(8,128)S(1)} %copy-done.7, bf16[8,128,768]{2,1,0:T(8,128)(2,1)} %bitcast.61, bf16[8,768,3072]{2,1,0:T(8,128)(2,1)} %param.8), kind=kOutput, calls=%fused_computation.24 | convolution fusion | flops 9693560832 | bytes 78647296 | tf_op jit(solution)/shard_map/ecf,efd->ecd/dot_general | solution.py:35
  129.4 0.0 copy-done.3
  129.4 0.0 copy-start.6
  129.4 9.4 %gather_fusion.4 = bf16[2048,768]{1,0:T(8,128)(2,1)} fusion(bf16[1024,768]{1,0:T(8,128)(2,1)S(1)} %bitcast.57, s32[2048]{0:T(1024)S(1)} %copy-done.3), kind=kCustom, calls=%fused_computation.4 | custom fusion | bytes 6299648 | tf_op jit(solution)/shard_map/gather | solution.py:37
  138.8 0.0 copy-done.6
  138.8 3.3 %broadcast_select_fusion = bf16[4,512,768]{2,1,0:T(8,128)(2,1)} fusion(bf16[4,512,768]{2,1,0:T(8,128)(2,1)} %bitcast.60, pred[4,512]{1,0:T(4,128)(4,1)S(1)} %copy-done.6), kind=kLoop, calls=%fused_computation.25 | loop fusion | flops 1572864 | bytes 6293504 | tf_op jit(solution)/shard_map/jit(_where)/select_n | solution.py:37
  142.1 0.0 copy-start.1
  142.1 4.8 %all-to-all-start.2 = ((bf16[4,512,768]{2,1,0:T(8,128)(2,1)}), bf16[4,512,768]{2,1,0:T(8,128)(2,1)}, u32[]{:S(2)}, u32[]{:S(2)}) async-start(bf16[4,512,768]{2,1,0:T(8,128)(2,1)} %broadcast_select_fusion), calls=%async_computation.2 | async-start | bytes 6291456 | tf_op jit(solution)/shard_map/all_to_all | solution.py:38
  146.9 0.0 copy-done.1
  146.9 1.9 convert_element_type.18
  148.9 34.7 %all-to-all-done.2 = bf16[4,512,768]{2,1,0:T(8,128)(2,1)} async-done(((bf16[4,512,768]{2,1,0:T(8,128)(2,1)}), bf16[4,512,768]{2,1,0:T(8,128)(2,1)}, u32[]{:S(2)}, u32[]{:S(2)}) %all-to-all-start.2) | async-done | bytes 3145760 | tf_op jit(solution)/shard_map/all_to_all | solution.py:38
  183.6 18.7 %scatter_custom_fusion.2 = f32[1024,768]{1,0:T(8,128)} fusion(f32[1024,768]{1,0:T(8,128)} %convert_element_type.18, s32[2048]{0:T(1024)} %bitcast.64, bf16[2048,768]{1,0:T(8,128)(2,1)} %bitcast.23), kind=kCustom, calls=%fused_computation.18 | custom fusion | flops 3145728 | bytes 6291456 | tf_op jit(solution)/shard_map/scatter-add | solution.py:39
  202.2 3.2 %convert_element_type.23 = bf16[1024,768]{1,0:T(8,128)(2,1)} convert(f32[1024,768]{1,0:T(8,128)} %scatter_custom_fusion.2) | non-fusion elementwise | flops 786432 | bytes 4718592 | tf_op jit(solution)/shard_map/convert_element_type | solution.py:40
  (11 shorter events, 0.1 us)
Async XLA Ops:
  14.4 13.0 %copy-start.4 = (s32[8,128]{1,0:T(8,128)S(1)}, s32[8,128]{1,0:T(8,128)}, u32[]{:S(2)}) copy-start(s32[8,128]{1,0:T(8,128)} %param.6) | copy-start | bytes 12292
  23.0 15.5 %copy-start.2 = (s32[2048]{0:T(1024)}, s32[2048]{0:T(1024)S(1)}, u32[]{:S(2)}) copy-start(s32[2048]{0:T(1024)S(1)} %broadcast_clamp_fusion.2) | copy-start | bytes 24580
  29.9 17.5 %copy-start = (bf16[1024,768]{1,0:T(8,128)(2,1)S(1)}, bf16[1024,768]{1,0:T(8,128)(2,1)}, u32[]{:S(2)}) copy-start(bf16[1024,768]{1,0:T(8,128)(2,1)} %param.5) | copy-start | bytes 4718596
  46.8 0.6 copy-start.5
  56.8 40.4 %all-to-all-start.1 = ((bf16[4,512,768]{2,1,0:T(8,128)(2,1)}), bf16[4,512,768]{2,1,0:T(8,128)(2,1)S(1)}, u32[]{:S(2)}, u32[]{:S(2)}) async-start(bf16[4,512,768]{2,1,0:T(8,128)(2,1)} %bitcast.59), calls=%async_computation.1 | async-start | bytes 6291456 | tf_op jit(solution)/shard_map/all_to_all | solution.py:31
  97.2 5.2 %copy-start.7 = (f32[8,128]{1,0:T(8,128)S(1)}, f32[8,128]{1,0:T(8,128)}, u32[]{:S(2)}) copy-start(f32[8,128]{1,0:T(8,128)} %param.7) | copy-start | bytes 12292
  102.4 27.0 %copy-start.3 = (s32[2048]{0:T(1024)S(1)}, s32[2048]{0:T(1024)}, u32[]{:S(2)}) copy-start(s32[2048]{0:T(1024)} %copy-done.2) | copy-start | bytes 24580
  129.4 9.4 %copy-start.6 = (pred[4,512]{1,0:T(4,128)(4,1)S(1)}, pred[4,512]{1,0:T(4,128)(4,1)}, u32[]{:S(2)}) copy-start(pred[4,512]{1,0:T(4,128)(4,1)} %iota_compare_fusion) | copy-start | bytes 6148
  142.1 4.8 %copy-start.1 = (bf16[1024,768]{1,0:T(8,128)(2,1)S(1)}, bf16[1024,768]{1,0:T(8,128)(2,1)}, u32[]{:S(2)}) copy-start(bf16[1024,768]{1,0:T(8,128)(2,1)} %param.5) | copy-start | bytes 4718596
  142.1 41.4 %all-to-all-start.2 = ((bf16[4,512,768]{2,1,0:T(8,128)(2,1)}), bf16[4,512,768]{2,1,0:T(8,128)(2,1)}, u32[]{:S(2)}, u32[]{:S(2)}) async-start(bf16[4,512,768]{2,1,0:T(8,128)(2,1)} %broadcast_select_fusion), calls=%async_computation.2 | async-start | bytes 6291456 | tf_op jit(solution)/shard_map/all_to_all | solution.py:38
where the time goes:
time: 206 us; the launch traced here: 205 us
  waiting for transfers between devices  70.7 us (34%)
  local copies, waits for them, and re-layouts  46.7 us (23%)
  other arithmetic  44.1 us (21%)
  matrix products  27 us (13%)
  starting transfers between devices  8.47 us (4%)
  blocking collectives  8.21 us (4%)
    all_to_all x1, waiting for transfers between devices, local_layer(): got_rows = lax.all_to_all(send_rows, 'ep', 0, 0, tiled=True)  36 us
    all_to_all x1, waiting for transfers between devices, local_layer(): returned = lax.all_to_all(back_rows, 'ep', 0, 0, tiled=True)  34.7 us
    dot_general x1, matrix products, local_layer(): jnp.einsum('ecf,efd->ecd', hidden, wout_loc, preferred_element_type=jnp.f...  27 us
    scatter-add x1, other arithmetic, local_layer(): jax.ops.segment_sum(returned.reshape(group_n * pair_cap, model_dim).astyp...  18.7 us
    gather x1, local copies, waits for them, and re-layouts, local_layer(): send_rows = tok_loc[asked_rows]  9.38 us
    gather x1, local copies, waits for them, and re-layouts, local_layer(): weighted[slot_of]  9.38 us
    gather x1, local copies, waits for them, and re-layouts, local_layer(): slot_order[jnp.minimum(starts[:, None] + lane_idx[None, :], slot_total - 1)]  8.58 us
    gather x1, local copies, waits for them, and re-layouts, local_layer(): request = jnp.where(is_valid, src_row[slot_of], 0)  8.58 us
  transfers between devices with their start and end apart: 2, of which 2 were waited for; matrix products, arithmetic and copies ran while one was open for 1% of the time, Pallas kernels for 0%

commit v1 on v0

v1 whole, which is shorter than its diff:
```python
import jax
import jax.numpy as jnp
from jax import lax
from jax.experimental import pallas as pl
from jax.experimental.pallas import tpu as pltpu
from jax.sharding import PartitionSpec as P

F32, BF16 = jnp.float32, jnp.bfloat16
W_SLOTS = 3
LANES = 128


def moe_kernel(tok, idx, gate, w_in, w_out, out,
               chip_tok, idx_all, gate_v, xsend, xrecv, xown, pbuf, acc, obuf, wi, wo,
               loc_sem, w_sem, idx_ss, idx_rs, tok_ss, tok_rs, x_ss, x_rs,
               po_ss, po_rs, pm_ss, pm_rs, pd_ss, pd_rs, out_sem):
    n_tok, d_model = tok.shape
    n_exp, cap = idx.shape
    d_ff = w_in.shape[2]
    ep = lax.axis_index("ep")
    chip, core = ep // 2, ep % 2
    mate = chip * 2 + (1 - core)
    opp = (1 - chip) * 2 + core
    diag = (1 - chip) * 2 + (1 - core)
    chip_base = chip * (2 * n_tok)

    def remote(src, dst, ss, rs, dev):
        return pltpu.make_async_remote_copy(src_ref=src, dst_ref=dst, send_sem=ss, recv_sem=rs,
                                            device_id={"ep": dev}, device_id_type=pl.DeviceIdType.MESH)

    def w_copies(e):
        slot = lax.rem(e, W_SLOTS)
        return (pltpu.make_async_copy(w_in.at[e], wi.at[slot], w_sem.at[0, slot]),
                pltpu.make_async_copy(w_out.at[e], wo.at[slot], w_sem.at[1, slot]))

    own_rows = pl.ds(pl.multiple_of(core * n_tok, n_tok), n_tok)
    own_tok = pltpu.make_async_copy(tok, chip_tok.at[own_rows], loc_sem.at[0])
    own_idx = pltpu.make_async_copy(idx, idx_all.at[ep], loc_sem.at[1])
    own_gate = pltpu.make_async_copy(gate, gate_v, loc_sem.at[2])
    own_tok.start()
    own_idx.start()
    own_gate.start()
    barrier = pltpu.get_barrier_semaphore()
    for dev in (mate, opp, diag):
        pl.semaphore_signal(barrier, inc=1, device_id={"ep": dev}, device_id_type=pl.DeviceIdType.MESH)
    pl.semaphore_wait(barrier, 3)

    idx_out = [remote(idx, idx_all.at[ep], idx_ss.at[k], idx_rs.at[k], dev) for k, dev in enumerate((opp, mate, diag))]
    tok_out = remote(tok, chip_tok.at[own_rows], tok_ss, tok_rs, mate)
    idx_out[0].start()
    tok_out.start()
    idx_out[1].start()
    idx_out[2].start()
    for e in range(W_SLOTS):
        for c in w_copies(e):
            c.start()

    lane = lax.broadcasted_iota(jnp.int32, (cap, LANES), 1)
    n_tiles = 2 * n_tok // LANES

    def gather(dev, e0, count):
        blocks = []
        for k in range(count):
            row = idx_all[dev, pl.ds(e0 + k, 1), :] - chip_base
            col = jnp.broadcast_to(row, (LANES, cap)).T
            tiles = [jnp.where(col == lane + LANES * j, 1.0, 0.0).astype(BF16) for j in range(n_tiles)]
            blocks.append(jnp.concatenate(tiles, axis=1))
        hot = jnp.concatenate(blocks, axis=0)
        return jnp.dot(hot, chip_tok[...], preferred_element_type=F32).astype(BF16)

    def rows_of(e, count=1):
        return pl.ds(pl.multiple_of(e * cap, cap), count * cap)

    def x_copy(e):
        return remote(xsend.at[rows_of(e)], xrecv.at[rows_of(e)], x_ss.at[e], x_rs.at[e], opp)

    own_tok.wait()
    own_idx.wait()
    idx_out[0].wait_recv()
    tok_out.wait_recv()

    @pl.loop(0, n_exp // 2)
    def _(g):
        xsend[rows_of(2 * g, 2), :] = gather(opp, 2 * g, 2)
        x_copy(2 * g).start()
        x_copy(2 * g + 1).start()

    @pl.loop(0, n_exp // 2)
    def _(g):
        xown[rows_of(2 * g, 2), :] = gather(ep, 2 * g, 2)

    own_gate.wait()

    @pl.loop(0, n_tok // 256)
    def _(b):
        r = pl.ds(pl.multiple_of(b * 256, 256), 256)
        acc[r, :] = chip_tok[pl.ds(pl.multiple_of(core * n_tok + b * 256, 256), 256), :].astype(F32)

    f_tile = 512

    def po_copy(e):
        return remote(pbuf.at[0, rows_of(e)], pbuf.at[2, rows_of(e)], po_ss.at[e], po_rs.at[e], opp)

    def pm_copy(e):
        return remote(pbuf.at[0, rows_of(e)], pbuf.at[1, rows_of(e)], pm_ss.at[e], pm_rs.at[e], mate)

    def pd_copy(e):
        return remote(pbuf.at[2, rows_of(e)], pbuf.at[3, rows_of(e)], pd_ss.at[e], pd_rs.at[e], mate)

    @pl.loop(0, n_exp)
    def _(e):
        slot = lax.rem(e, W_SLOTS)
        x_copy(e).wait_recv()
        x = xrecv[rows_of(e), :] + xown[rows_of(e), :]
        for c in w_copies(e):
            c.wait()
        o = None
        for f in range(d_ff // f_tile):
            fs = slice(f * f_tile, (f + 1) * f_tile)
            pre = jnp.dot(x, wi[slot, :, fs], preferred_element_type=F32)
            h = jax.nn.gelu(pre, approximate=True).astype(BF16)
            part = jnp.dot(h, wo[slot, fs, :], preferred_element_type=F32)
            o = part if o is None else o + part
        gcol = jnp.broadcast_to(gate_v[pl.ds(e, 1), :], (LANES, cap)).T
        pbuf[0, rows_of(e), :] = (jnp.concatenate([gcol] * (d_model // LANES), axis=1) * o).astype(BF16)
        po_copy(e).start()
        pm_copy(e).start()

        @pl.when(e + W_SLOTS < n_exp)
        def _():
            for c in w_copies(e + W_SLOTS):
                c.start()

    idx_out[1].wait_recv()
    idx_out[2].wait_recv()

    n_blk = n_tok // 256
    sub = lax.broadcasted_iota(jnp.int32, (256, cap), 0)

    def scatter(e, last):
        rows = [idx_all[dev, pl.ds(e, 1), :] - ep * n_tok for dev in (ep, mate, opp, diag)]
        pcat = jnp.concatenate([pbuf[k, rows_of(e), :] for k in range(4)], axis=0)

        def block(b):
            r = pl.ds(pl.multiple_of(b * 256, 256), 256)
            hot = jnp.concatenate(
                [jnp.where(row == sub + b * 256, 1.0, 0.0).astype(BF16) for row in rows], axis=1)
            total = acc[r, :] + jnp.dot(hot, pcat, preferred_element_type=F32)
            if last:
                obuf[r, :] = total.astype(BF16)
                pltpu.make_async_copy(obuf.at[r], out.at[r], out_sem.at[b]).start()
            else:
                acc[r, :] = total

        pl.loop(0, n_blk)(block)

    def combine(e, last):
        po_copy(e).wait_recv()
        pd_copy(e).start()
        pm_copy(e).wait_recv()
        pd_copy(e).wait_recv()
        scatter(e, last)

    @pl.loop(0, n_exp - 1)
    def _(e):
        combine(e, False)

    combine(n_exp - 1, True)

    for c in idx_out:
        c.wait_send()
    tok_out.wait_send()

    @pl.loop(0, n_exp)
    def _(e):
        x_copy(e).wait_send()
        po_copy(e).wait_send()
        pm_copy(e).wait_send()
        pd_copy(e).wait_send()

    @pl.loop(0, n_blk)
    def _(b):
        r = pl.ds(pl.multiple_of(b * 256, 256), 256)
        pltpu.make_async_copy(obuf.at[r], out.at[r], out_sem.at[b]).wait()


def solution(mesh):
    row_spec = P(("dp", "ep"), None)
    expert_spec = P("ep", None, None)

    def local_layer(tok, idx, gate, w_in, w_out):
        n_tok, d_model = tok.shape
        n_exp, cap = idx.shape
        d_ff = w_in.shape[2]
        slots = n_exp * cap
        dma = pltpu.SemaphoreType.DMA
        any_spec = pl.BlockSpec(memory_space=pl.ANY)
        return pl.pallas_call(
            moe_kernel,
            out_shape=jax.ShapeDtypeStruct((n_tok, d_model), BF16),
            in_specs=[any_spec] * 5,
            out_specs=any_spec,
            scratch_shapes=[
                pltpu.VMEM((2 * n_tok, d_model), BF16),
                pltpu.VMEM((4, n_exp, cap), jnp.int32),
                pltpu.VMEM((n_exp, cap), F32),
                pltpu.VMEM((slots, d_model), BF16),
                pltpu.VMEM((slots, d_model), BF16),
                pltpu.VMEM((slots, d_model), BF16),
                pltpu.VMEM((4, slots, d_model), BF16),
                pltpu.VMEM((n_tok, d_model), F32),
                pltpu.VMEM((n_tok, d_model), BF16),
                pltpu.VMEM((W_SLOTS, d_model, d_ff), BF16),
                pltpu.VMEM((W_SLOTS, d_ff, d_model), BF16),
                dma((3,)), dma((2, W_SLOTS)), dma((3,)), dma((3,)), dma, dma,
                dma((n_exp,)), dma((n_exp,)), dma((n_exp,)), dma((n_exp,)),
                dma((n_exp,)), dma((n_exp,)), dma((n_exp,)), dma((n_exp,)),
                dma((n_tok // 256,)),
            ],
            compiler_params=pltpu.CompilerParams(
                collective_id=0, has_side_effects=True, vmem_limit_bytes=63 * 1024 * 1024),
        )(tok, idx, gate, w_in, w_out)

    return jax.shard_map(local_layer, mesh=mesh, in_specs=(row_spec, row_spec, row_spec, expert_spec, expert_spec),
                         out_specs=row_spec, check_vma=False)
```

time: 206 us -> 82.5 us (0.40)
  Pallas kernels: 0 us -> 79.7 us
  waiting for transfers between devices: 70.7 us -> 0 us
  other arithmetic: 44.1 us -> 0 us
  local copies, waits for them, and re-layouts: 46.7 us -> 2.65 us
  matrix products: 27 us -> 0 us
  starting transfers between devices: 8.47 us -> 0 us
  blocking collectives: 8.21 us -> 0 us
    pallas_call x0 -> x1, Pallas kernels: none -> 79.7 us  [local_layer(): pl.pallas_call(moe_kernel, out_shape=jax.ShapeDtypeStruct((n_tok, d_model...]
    all_to_all x2 -> x0, waiting for transfers between devices: 70.7 us -> none  [the longest x1 36 us: local_layer(): got_rows = lax.all_to_all(send_rows, 'ep', 0, 0, tiled=True)]
    gather x6 -> x0, local copies, waits for them, and re-layouts: 41.8 us -> none  [the longest x1 9.38 us: local_layer(): send_rows = tok_loc[asked_rows]]
    dot_general x1 -> x0, matrix products: 27 us -> none  [local_layer(): jnp.einsum('ecf,efd->ecd', hidden, wout_loc, preferred_element_type=jnp.f...]
    scatter-add x2 -> x0, other arithmetic: 26.3 us -> none  [the longest x1 18.7 us: local_layer(): jax.ops.segment_sum(returned.reshape(group_n * pair_cap, model_dim).astyp...]
    all_to_all x2 -> x0, starting transfers between devices: 8.47 us -> none  [the longest x1 4.77 us: local_layer(): returned = lax.all_to_all(back_rows, 'ep', 0, 0, tiled=True)]
    all_to_all x1 -> x0, blocking collectives: 8.21 us -> none  [local_layer(): asked_rows = lax.all_to_all(request, 'ep', 0, 0, tiled=True)]
    convert_element_type x2 -> x0, other arithmetic: 5.12 us -> none  [local_layer(): return (tok_loc.astype(jnp.float32) + added).astype(jnp.bfloat16)]
  transfers between devices with their start and end apart: 2 -> 0, of which waited for: 2 -> 0; matrix products, arithmetic and copies ran while one was open for 1% -> 0% of each run, Pallas kernels for 0% -> 0%
where the time goes in v1:
time: 82.5 us; the launch traced here: 82.3 us
  Pallas kernels  79.7 us (97%)
  local copies, waits for them, and re-layouts  2.65 us (3%)
    pallas_call x1, Pallas kernels, local_layer(): pl.pallas_call(moe_kernel, out_shape=jax.ShapeDtypeStruct((n_tok, d_model...  79.7 us
    unnamed x1, local copies, waits for them, and re-layouts  2.65 us

profile of v1, /device:TPU:0, one launch (start us, length us, event | category | flops | bytes accessed | tf_op | source)
XLA Modules:
  0.0 82.3 jit_solution(11169480881278341275)
XLA Ops:
  0.0 79.7 %shard_map.55 = bf16[1024,768]{1,0:T(8,128)(2,1)} custom-call(bf16[1024,768]{1,0:T(8,128)(2,1)} %tok.1, s32[8,128]{1,0:T(8,128)} %idx.1, f32[8,128]{1,0:T(8,128)} %gate.1, bf16[8,768,3072]{2,1,0:T(8,128)(2,1)} %w_in.1, bf16[8,3072,768]{2,1,0:T(8,128)(2,1)} %w_out.1), custom_call_target="tpu_custom_call" | custom-call | tf_op jit(solution)/shard_map/pallas_call | solution.py:198
  79.7 2.7 %copy.7 = bf16[1024,768]{1,0:T(8,128)(2,1)} copy(bf16[1024,768]{1,0:T(8,128)(2,1)} %shard_map.55) | data formatting | bytes 3145728

commit v2 on v0

v2 whole, which is shorter than its diff:
```python
import functools

import jax
import jax.numpy as jnp
from jax import lax
from jax.experimental import pallas as pl
from jax.experimental.pallas import tpu as pltpu
from jax.sharding import PartitionSpec as P

F32, BF16, I32 = jnp.float32, jnp.bfloat16, jnp.int32
W_SLOTS = 3
LANES = 128
FAR = 1 << 20


def remote(src, dst, ss, rs, **dev):
    return pltpu.make_async_remote_copy(src_ref=src, dst_ref=dst, send_sem=ss, recv_sem=rs,
                                        device_id=dev, device_id_type=pl.DeviceIdType.MESH)


def signal(sem, **dev):
    pl.semaphore_signal(sem, inc=1, device_id=dev, device_id_type=pl.DeviceIdType.MESH)


def plan_kernel(n_dp, n_ep, sizes, tok, idx, mate_tok, meta, bucket, idx_g, loc_sem, idx_ss, idx_rs, tok_ss, tok_rs):
    n_tok = tok.shape[0]
    n_exp, cap = idx.shape
    dp, ep = lax.axis_index("dp"), lax.axis_index("ep")
    me = dp * n_ep + ep
    n_dev = n_dp * n_ep
    own_idx = pltpu.make_async_copy(idx, idx_g.at[me], loc_sem)
    own_idx.start()
    barrier = pltpu.get_barrier_semaphore()
    others = []
    for k in range(1, n_dev):
        dev = lax.rem(me + k, n_dev)
        others.append((dev // n_ep, lax.rem(dev, n_ep)))
    for d, e in others:
        signal(barrier, dp=d, ep=e)
    pl.semaphore_wait(barrier, n_dev - 1)
    mate = ep + 1 - 2 * lax.rem(ep, 2)
    tok_out = remote(tok, mate_tok, tok_ss, tok_rs, dp=dp, ep=mate)
    tok_out.start()
    own_idx.wait()
    sends = []
    for k, (d, e) in enumerate(others):
        c = remote(idx_g.at[me], idx_g.at[me], idx_ss.at[k], idx_rs.at[k], dp=d, ep=e)
        c.start()
        sends.append(c)
    rows = 2 * n_exp
    half = 2 * n_tok

    key_r = lax.broadcasted_iota(I32, (rows, rows), 0)
    key_c = lax.broadcasted_iota(I32, (rows, rows), 1)
    order_r = lax.rem(key_r, n_exp) * 2 + key_r // n_exp
    order_c = lax.rem(key_c, n_exp) * 2 + key_c // n_exp
    before = jnp.where(order_c < order_r, 1.0, 0.0).astype(BF16)
    every = jnp.ones((rows, rows), BF16)
    up_r = lax.broadcasted_iota(I32, (cap, cap), 0)
    up_c = lax.broadcasted_iota(I32, (cap, cap), 1)
    upper = jnp.where(up_r < up_c, 1.0, 0.0).astype(BF16)
    ones = jnp.ones((cap, cap), BF16)

    for c in sends:
        c.wait_recv()

    def crosses(d, h):
        ids = jnp.concatenate([idx_g[d * n_ep + 2 * h], idx_g[d * n_ep + 2 * h + 1]], axis=0)
        return ids, (ids >= half) if h == 0 else (ids < half)

    most = None
    for d in range(n_dp):
        for h in range(2):
            _, need = crosses(d, h)
            n = jnp.sum(jnp.where(need, 1.0, 0.0))
            most = n if most is None else jnp.maximum(most, n)
    pick = jnp.int32(0)
    for s in sizes[:-1]:
        pick = pick + jnp.where(most > s, 1, 0).astype(I32)
    bucket[0] = pick

    for h in range(2):
        ids, need = crosses(dp, h)
        flag = jnp.where(need, 1.0, 0.0).astype(BF16)
        in_row = jnp.dot(flag, upper, preferred_element_type=F32)
        row_sum = jnp.dot(flag, ones, preferred_element_type=F32).astype(BF16)
        prior = jnp.dot(before, row_sum, preferred_element_type=F32)
        total = jnp.dot(every, row_sum, preferred_element_type=F32)
        pos = (in_row + prior).astype(I32)
        meta[0, h * rows:(h + 1) * rows, :] = ids
        meta[1, h * rows:(h + 1) * rows, :] = jnp.where(need, pos, FAR)
        meta[2, h * rows:(h + 1) * rows, :] = jnp.where(need, pos - total.astype(I32), FAR)

    for c in sends:
        c.wait_send()
    tok_out.wait()


def layer_kernel(k_rows, tok, mate_tok, meta, gate, w_in, w_out, out,
                 chip_tok, meta_v, gate_v, xsend, land, local, xbuf, chip_p, pland, rsend, rland, tokrow,
                 acc, obuf, wi, wo,
                 loc_sem, w_sem, d_ss, d_rs, f_ss, f_rs, p_ss, p_rs, r_ss, r_rs, g_ss, g_rs, out_sem):
    n_tok, d_model = tok.shape
    n_exp, d_ff = w_in.shape[0], w_in.shape[2]
    cap = gate.shape[1]
    slots = n_exp * cap
    rows = 2 * n_exp
    nc = k_rows // (2 * cap)
    ep = lax.axis_index("ep")
    chip, core = ep // 2, ep % 2
    mate = chip * 2 + (1 - core)
    opp = (1 - chip) * 2 + core
    chip_base = chip * (2 * n_tok)

    def at(start, size):
        return pl.ds(pl.multiple_of(start, cap), size)

    def w_copies(e):
        slot = lax.rem(e, W_SLOTS)
        return (pltpu.make_async_copy(w_in.at[e], wi.at[slot], w_sem.at[0, slot]),
                pltpu.make_async_copy(w_out.at[e], wo.at[slot], w_sem.at[1, slot]))

    first = [pltpu.make_async_copy(meta, meta_v, loc_sem.at[0]),
             pltpu.make_async_copy(tok, chip_tok.at[at(core * n_tok, n_tok)], loc_sem.at[1]),
             pltpu.make_async_copy(mate_tok, chip_tok.at[at((1 - core) * n_tok, n_tok)], loc_sem.at[2]),
             pltpu.make_async_copy(gate, gate_v, loc_sem.at[3])]
    for c in first:
        c.start()
    barrier = pltpu.get_barrier_semaphore()
    signal(barrier, ep=mate)
    signal(barrier, ep=opp)
    for e in range(W_SLOTS):
        for c in w_copies(e):
            c.start()

    def d_copy(m):
        return remote(xsend.at[at(m * cap, cap)], land.at[at((2 * m + core) * cap, cap)], d_ss.at[m], d_rs.at[m], ep=opp)

    def f_copy(m):
        r = at((2 * m + core) * cap, cap)
        return remote(land.at[r], land.at[r], f_ss.at[m], f_rs.at[m], ep=mate)

    def p_copy(e):
        return remote(chip_p.at[at(core * slots + e * cap, cap)], pland.at[at(e * cap, cap)], p_ss.at[e], p_rs.at[e], ep=mate)

    def r_copy(m):
        return remote(rsend.at[at(m * cap, cap)], rland.at[at((2 * m + core) * cap, cap)], r_ss.at[m], r_rs.at[m], ep=opp)

    def g_copy(m):
        r = at((2 * m + core) * cap, cap)
        return remote(rland.at[r], rland.at[r], g_ss.at[m], g_rs.at[m], ep=mate)

    lane = lax.broadcasted_iota(I32, (cap, LANES), 1)
    sub = lax.broadcasted_iota(I32, (cap, LANES), 0)

    def spread(col, width, base):
        return jnp.concatenate(
            [jnp.where(col == lane + (base + LANES * j), 1.0, 0.0).astype(BF16) for j in range(width // LANES)], axis=1)

    def column(row):
        return jnp.broadcast_to(row, (LANES, cap)).T

    their = (1 - chip) * rows
    mine = chip * rows

    def owner_ids(kind, block, shift):
        t = jnp.zeros((cap, LANES), I32)
        for i in range(rows):
            pos = meta_v[kind, pl.ds(their + i, 1), :] + shift
            ids = meta_v[0, pl.ds(their + i, 1), :]
            t = t + jnp.where(jnp.broadcast_to(pos, (cap, LANES)) == sub + block * cap, jnp.broadcast_to(ids, (cap, LANES)), 0)
        return t

    first[0].wait()

    def gather_block(m):
        t = owner_ids(1, 2 * m + core, 0).astype(F32)
        ids = jnp.sum(t, axis=1, keepdims=True).astype(I32) - chip_base
        return spread(jnp.broadcast_to(ids, (cap, LANES)), 2 * n_tok, 0)

    first[1].wait()
    first[2].wait()
    pl.semaphore_wait(barrier, 2)

    def send_group(m0, count):
        hot = jnp.concatenate([gather_block(m0 + k) for k in range(count)], axis=0)
        xsend[at(m0 * cap, count * cap), :] = jnp.dot(hot, chip_tok[...], preferred_element_type=F32).astype(BF16)
        for k in range(count):
            d_copy(m0 + k).start()

    @pl.loop(0, nc // 2)
    def _(g):
        send_group(2 * g, 2)

    if nc % 2:
        send_group(nc - 1, 1)

    @pl.loop(0, n_exp // 2)
    def _(g):
        hot = jnp.concatenate(
            [spread(column(meta_v[0, pl.ds(mine + core * n_exp + 2 * g + k, 1), :] - chip_base), 2 * n_tok, 0)
             for k in range(2)], axis=0)
        xbuf[at(2 * g * cap, 2 * cap), :] = jnp.dot(hot, chip_tok[...], preferred_element_type=F32).astype(BF16)

    @pl.loop(0, 2 * nc)
    def _(j):
        t = owner_ids(2, j, k_rows).astype(F32).T
        tokrow[pl.ds(j, 1), :] = jnp.sum(t, axis=0, keepdims=True).astype(I32)

    @pl.loop(0, k_rows // (2 * cap))
    def _(b):
        local[at(b * 2 * cap, 2 * cap), :] = jnp.zeros((2 * cap, d_model), BF16)

    @pl.loop(0, rows // 2)
    def _(b):
        chip_p[at(b * 2 * cap, 2 * cap), :] = jnp.zeros((2 * cap, d_model), BF16)

    first[3].wait()

    def forward(m):
        d_copy(m).wait_recv()
        f_copy(m).start()

    forward(0)
    if nc > 1:
        forward(1)
    f_tile = 512

    def pack_return(e):
        p_copy(e).wait_recv()
        chip_p[at((1 - core) * slots + e * cap, cap), :] = pland[at(e * cap, cap), :]
        m = e - (n_exp - nc)

        @pl.when(m >= 0)
        def _():
            parts = []
            for i in range(rows):
                pos = meta_v[2, pl.ds(mine + i, 1), :] + k_rows
                parts.append(jnp.where(jnp.broadcast_to(pos, (cap, LANES)) == sub + (2 * m + core) * cap, 1.0, 0.0).astype(BF16))
            hot = jnp.concatenate(parts, axis=1)
            rsend[at(m * cap, cap), :] = jnp.dot(hot, chip_p[...], preferred_element_type=F32).astype(BF16)
            r_copy(m).start()

    @pl.loop(0, n_exp)
    def _(e):
        slot = lax.rem(e, W_SLOTS)

        @pl.when(lax.rem(e, 2) == 0)
        def _():
            for k in range(2):
                m = e + k

                @pl.when(m < nc)
                def _():
                    f_copy(m).wait_recv()
                    local[at(2 * m * cap, 2 * cap), :] = land[at(2 * m * cap, 2 * cap), :]

            hot = jnp.concatenate(
                [spread(column(meta_v[1, pl.ds(mine + core * n_exp + e + k, 1), :]), k_rows, 0) for k in range(2)], axis=0)
            r = at(e * cap, 2 * cap)
            xbuf[r, :] = xbuf[r, :] + jnp.dot(hot, local[...], preferred_element_type=F32).astype(BF16)

        x = xbuf[at(e * cap, cap), :]
        for c in w_copies(e):
            c.wait()
        o = None
        for f in range(d_ff // f_tile):
            fs = slice(f * f_tile, (f + 1) * f_tile)
            pre = jnp.dot(x, wi[slot, :, fs], preferred_element_type=F32)
            h = jax.nn.gelu(pre, approximate=True).astype(BF16)
            part = jnp.dot(h, wo[slot, fs, :], preferred_element_type=F32)
            o = part if o is None else o + part
        gcol = column(gate_v[pl.ds(e, 1), :])
        chip_p[at(core * slots + e * cap, cap), :] = (jnp.concatenate([gcol] * (d_model // LANES), axis=1) * o).astype(BF16)
        p_copy(e).start()

        @pl.when(e + W_SLOTS < n_exp)
        def _():
            for c in w_copies(e + W_SLOTS):
                c.start()

        @pl.when(e + 2 < nc)
        def _():
            forward(e + 2)

        @pl.when(e > 0)
        def _():
            pack_return(e - 1)

    pack_return(n_exp - 1)

    n_blk = n_tok // (2 * cap)
    blk = 2 * cap
    sub_b = lax.broadcasted_iota(I32, (blk, LANES), 0) + ep * n_tok

    @pl.loop(0, n_blk)
    def _(b):
        r = at(b * blk, blk)
        hot = jnp.concatenate(
            [jnp.where(jnp.broadcast_to(meta_v[0, pl.ds(mine + i, 1), :], (blk, LANES)) == sub_b + b * blk, 1.0, 0.0).astype(BF16)
             for i in range(rows)], axis=1)
        own = chip_tok[at(core * n_tok + b * blk, blk), :].astype(F32)
        acc[r, :] = own + jnp.dot(hot, chip_p[...], preferred_element_type=F32)

    def combine(m, last):
        r_copy(m).wait_recv()
        g_copy(m).start()
        ids = [tokrow[pl.ds(2 * m + k, 1), :] for k in range(2)]
        g_copy(m).wait_recv()
        back = rland[at(2 * m * cap, 2 * cap), :]

        @pl.loop(0, n_blk)
        def _(b):
            r = at(b * blk, blk)
            hot = jnp.concatenate(
                [jnp.where(jnp.broadcast_to(i, (blk, LANES)) == sub_b + b * blk, 1.0, 0.0).astype(BF16) for i in ids], axis=1)
            total = acc[r, :] + jnp.dot(hot, back, preferred_element_type=F32)
            if last:
                obuf[r, :] = total.astype(BF16)
                pltpu.make_async_copy(obuf.at[r], out.at[r], out_sem.at[b]).start()
            else:
                acc[r, :] = total

    @pl.loop(0, nc - 1)
    def _(m):
        combine(m, False)

    combine(nc - 1, True)

    @pl.loop(0, nc)
    def _(m):
        d_copy(m).wait_send()
        f_copy(m).wait_send()
        r_copy(m).wait_send()
        g_copy(m).wait_send()

    @pl.loop(0, n_exp)
    def _(e):
        p_copy(e).wait_send()

    @pl.loop(0, n_blk)
    def _(b):
        r = at(b * blk, blk)
        pltpu.make_async_copy(obuf.at[r], out.at[r], out_sem.at[b]).wait()


def solution(mesh):
    n_dp, n_ep = mesh.shape["dp"], mesh.shape["ep"]
    row_spec = P(("dp", "ep"), None)
    expert_spec = P("ep", None, None)
    dma = pltpu.SemaphoreType.DMA
    any_spec = pl.BlockSpec(memory_space=pl.ANY)

    def local_layer(tok, idx, gate, w_in, w_out):
        n_tok, d_model = tok.shape
        n_exp, cap = idx.shape
        d_ff = w_in.shape[2]
        slots = n_exp * cap
        sizes = tuple(slots + i * 2 * cap for i in range(slots // (2 * cap) + 1))
        n_dev = n_dp * n_ep

        mate_tok, meta, bucket = pl.pallas_call(
            functools.partial(plan_kernel, n_dp, n_ep, sizes),
            out_shape=(jax.ShapeDtypeStruct((n_tok, d_model), BF16),
                       jax.ShapeDtypeStruct((3, 4 * n_exp, cap), I32),
                       jax.ShapeDtypeStruct((1,), I32)),
            in_specs=[any_spec] * 2,
            out_specs=(any_spec, pl.BlockSpec(memory_space=pltpu.VMEM), pl.BlockSpec(memory_space=pltpu.SMEM)),
            scratch_shapes=[
                pltpu.VMEM((n_dev, n_exp, cap), I32),
                dma, dma((n_dev - 1,)), dma((n_dev - 1,)), dma, dma,
            ],
            compiler_params=pltpu.CompilerParams(collective_id=0, has_side_effects=True),
        )(tok, idx)

        def branch(i):
            k_rows = sizes[i]
            nc = k_rows // (2 * cap)

            def run(tok, mate_tok, meta, gate, w_in, w_out):
                return pl.pallas_call(
                    functools.partial(layer_kernel, k_rows),
                    out_shape=jax.ShapeDtypeStruct((n_tok, d_model), BF16),
                    in_specs=[any_spec] * 6,
                    out_specs=any_spec,
                    scratch_shapes=[
                        pltpu.VMEM((2 * n_tok, d_model), BF16),
                        pltpu.VMEM((3, 4 * n_exp, cap), I32),
                        pltpu.VMEM((n_exp, cap), F32),
                        pltpu.VMEM((nc * cap, d_model), BF16),
                        pltpu.VMEM((k_rows, d_model), BF16),
                        pltpu.VMEM((k_rows, d_model), BF16),
                        pltpu.VMEM((slots, d_model), BF16),
                        pltpu.VMEM((2 * slots, d_model), BF16),
                        pltpu.VMEM((slots, d_model), BF16),
                        pltpu.VMEM((nc * cap, d_model), BF16),
                        pltpu.VMEM((k_rows, d_model), BF16),
                        pltpu.VMEM((2 * nc, cap), I32),
                        pltpu.VMEM((n_tok, d_model), F32),
                        pltpu.VMEM((n_tok, d_model), BF16),
                        pltpu.VMEM((W_SLOTS, d_model, d_ff), BF16),
                        pltpu.VMEM((W_SLOTS, d_ff, d_model), BF16),
                        dma((4,)), dma((2, W_SLOTS)),
                        dma((nc,)), dma((nc,)), dma((nc,)), dma((nc,)),
                        dma((n_exp,)), dma((n_exp,)),
                        dma((nc,)), dma((nc,)), dma((nc,)), dma((nc,)),
                        dma((n_tok // (2 * cap),)),
                    ],
                    compiler_params=pltpu.CompilerParams(
                        collective_id=1 + i, has_side_effects=True, vmem_limit_bytes=63 * 1024 * 1024),
                )(tok, mate_tok, meta, gate, w_in, w_out)

            return run

        return lax.switch(bucket[0], [branch(i) for i in range(len(sizes))], tok, mate_tok, meta, gate, w_in, w_out)

    return jax.shard_map(local_layer, mesh=mesh, in_specs=(row_spec, row_spec, row_spec, expert_spec, expert_spec),
                         out_specs=row_spec, check_vma=False)
```

time: 206 us -> 77.2 us (0.37)
  Pallas kernels: 0 us -> 73.2 us
  waiting for transfers between devices: 70.7 us -> 0 us
  other arithmetic: 44.1 us -> 0 us
  local copies, waits for them, and re-layouts: 46.7 us -> 2.66 us
  matrix products: 27 us -> 0 us
  starting transfers between devices: 8.47 us -> 0 us
  blocking collectives: 8.21 us -> 0 us
    pallas_call x0 -> x2, Pallas kernels: none -> 73.2 us  [the longest x1 64.8 us: run(): pl.pallas_call(functools.partial(layer_kernel, k_rows), out_shape=jax.Sha...]
    all_to_all x2 -> x0, waiting for transfers between devices: 70.7 us -> none  [the longest x1 36 us: local_layer(): got_rows = lax.all_to_all(send_rows, 'ep', 0, 0, tiled=True)]
    gather x6 -> x0, local copies, waits for them, and re-layouts: 41.8 us -> none  [the longest x1 9.38 us: local_layer(): send_rows = tok_loc[asked_rows]]
    dot_general x1 -> x0, matrix products: 27 us -> none  [local_layer(): jnp.einsum('ecf,efd->ecd', hidden, wout_loc, preferred_element_type=jnp.f...]
    scatter-add x2 -> x0, other arithmetic: 26.3 us -> none  [the longest x1 18.7 us: local_layer(): jax.ops.segment_sum(returned.reshape(group_n * pair_cap, model_dim).astyp...]
    all_to_all x2 -> x0, starting transfers between devices: 8.47 us -> none  [the longest x1 4.77 us: local_layer(): returned = lax.all_to_all(back_rows, 'ep', 0, 0, tiled=True)]
    all_to_all x1 -> x0, blocking collectives: 8.21 us -> none  [local_layer(): asked_rows = lax.all_to_all(request, 'ep', 0, 0, tiled=True)]
    convert_element_type x2 -> x0, other arithmetic: 5.12 us -> none  [local_layer(): return (tok_loc.astype(jnp.float32) + added).astype(jnp.bfloat16)]
  transfers between devices with their start and end apart: 2 -> 0, of which waited for: 2 -> 0; matrix products, arithmetic and copies ran while one was open for 1% -> 0% of each run, Pallas kernels for 0% -> 0%
where the time goes in v2:
time: 77.2 us; the launch traced here: 77 us
  Pallas kernels  73.2 us (95%)
  local copies, waits for them, and re-layouts  2.66 us (3%)
    pallas_call x1, Pallas kernels, run(): pl.pallas_call(functools.partial(layer_kernel, k_rows), out_shape=jax.Sha...  64.8 us
    pallas_call x1, Pallas kernels, local_layer(): pl.pallas_call(functools.partial(plan_kernel, n_dp, n_ep, sizes), out_sha...  8.41 us
    unnamed x3, local copies, waits for them, and re-layouts  2.66 us

profile of v2, /device:TPU:0, one launch (start us, length us, event | category | flops | bytes accessed | tf_op | source)
XLA Modules:
  0.0 77.0 jit_solution(13703137158622080847)
XLA Ops:
  0.0 0.0 copy-start
  0.0 8.4 %shard_map.60 = (bf16[1024,768]{1,0:T(8,128)(2,1)}, s32[3,32,128]{2,1,0:T(8,128)S(1)}, s32[1]{0:T(128)}) custom-call(bf16[1024,768]{1,0:T(8,128)(2,1)} %tok.1, s32[8,128]{1,0:T(8,128)} %idx.1), custom_call_target="tpu_custom_call" | custom-call | tf_op jit(solution)/shard_map/pallas_call | solution.py:362
  9.1 0.0 copy-done
  9.1 65.3 %conditional.1 = (bf16[1024,768]{1,0:T(8,128)(2,1)}) conditional(s32[]{:T(128)} %bitcast, (bf16[1024,768]{1,0:T(8,128)(2,1)}, bf16[1024,768]{1,0:T(8,128)(2,1)}, s32[3,32,128]{2,1,0:T(8,128)S(1)}, f32[8,128]{1,0:T(8,128)S(1)}, bf16[8,768,3072]{2,1,0:T(8,128)(2,1)}, ...), branch_computations={%region_0.0_spmd, %region_1.0_spmd, %region_2.0_spmd, %region_3.0_... | conditional | bytes 8 | solution.py:415
  9.3 64.8 %branch_2_fun.1 = bf16[1024,768]{1,0:T(8,128)(2,1)} custom-call(bf16[1024,768]{1,0:T(8,128)(2,1)} %get-tuple-element.83.tok, bf16[1024,768]{1,0:T(8,128)(2,1)} %get-tuple-element.84.mate_tok, s32[3,32,128]{2,1,0:T(8,128)S(1)} %get-tuple-element.85.meta, f32[8,128]{1,0:T(8,128)S(1)} %get-tuple-element.86.gate, bf16[8,768,3072]{2,1,0:T(8,128)(2,1)} %get-tuple-element.87.w_in, ...), custom_call_target="tpu_custom_call" | custom-call | tf_op jit(solution)/shard_map/cond/branch_2_fun/pallas_call | solution.py:381
  74.4 2.7 %copy.17 = bf16[1024,768]{1,0:T(8,128)(2,1)} copy(bf16[1024,768]{1,0:T(8,128)(2,1)} %get-tuple-element.107) | data formatting | bytes 3145728
Async XLA Ops:
  0.0 9.1 %copy-start = (f32[8,128]{1,0:T(8,128)S(1)}, f32[8,128]{1,0:T(8,128)}, u32[]{:S(2)}) copy-start(f32[8,128]{1,0:T(8,128)} %param.12) | copy-start | bytes 12292
